TPU v7x, 512 devices: a whole 4x8x8 slice. The times are simulated.
512 devices in a mesh: freq: 8 (over z), tile: 64 (over y, x, core).
Axes of the slice: x: 4, y: 8, z: 8, core: 2. Of those that a mesh axis runs over, the one named last changes fastest.
Arguments:
- left_factor: bfloat16 [16, 8192, 32, 128], P('freq', 'tile'), may hold values from -0.09375 to 0.09375
- right_factor: bfloat16 [16, 8192, 32, 128], P('freq', 'tile'), may hold values from -0.25 to 0.25
- tile_ranks: int32 [16, 32, 32], P('freq'), may hold values from 16 to 64, as said below
- freq_order: int32 [16], replicated, may hold values from 0 to 15, each once
- mute_window: int32 [8192, 64], P(('tile', 'freq')), may hold values from 2 to 31
- direct_wave: float32 [16, 2, 8192, 64], P('freq', None, 'tile'), may hold values from -6 to 6
Outputs:
- focusing_plus: float32 [16, 2, 8192, 64], P('freq', None, 'tile')
- focusing_minus: float32 [16, 2, 8192, 64], P('freq', None, 'tile')
Inputs may be any that keep to these rules, and one draw needn't show every extreme that they name: tile_ranks[m, i, j] is the rank of tile (i, j) in slot m; every slot has a tile of rank 64. `freq_order`: each frequency index appears in one slot.
All inputs are finite; a program needn't handle non-finite values.
Results may differ from a plain program's by a relative error of at most 0.0051.
Values may be sent and summed in bfloat16 or wider, within the bound.
A program may use at most 64 MiB of HBM per device.

v0:
```python
import math

import jax
import jax.numpy as jnp
from jax import lax
from jax.sharding import PartitionSpec as P

TILE = 256
PANEL = 128
FREQS = 16
SAMPLES = 32


def from_partner(value, axis, bit):
    mask = 2**bit
    pairs = [(source, source ^ mask) for source in range(lax.axis_size(axis))]
    return lax.ppermute(value, axis, pairs)


def transform_tables(freq_order):
    angular = (freq_order.astype(jnp.float32) + 0.5) * (2.0 * math.pi / SAMPLES)
    sample_times = jnp.arange(SAMPLES, dtype=jnp.float32)
    phases = sample_times[:, None] * angular[None, :]
    columns = jnp.stack([jnp.cos(phases), -jnp.sin(phases)], axis=2).reshape(SAMPLES, 2 * FREQS)
    return (columns * (2.0 / SAMPLES), columns.T)


def combine(products, signum):
    rank_most = products.shape[-2] // 2
    focal_count = products.shape[-1] // 2
    real_real = products[..., :rank_most, :focal_count]
    real_imag = products[..., :rank_most, focal_count:]
    imag_real = products[..., rank_most:, :focal_count]
    imag_imag = products[..., rank_most:, focal_count:]
    return jnp.concatenate(
        [real_real - signum * imag_imag, real_imag + signum * imag_real], axis=-1
    )


def prepare(inner_factor, fields, signum, ranks_oriented):
    freq_count, row_count, block_count, rank_width = inner_factor.shape
    rank_most = rank_width // 2
    focal_count = fields.shape[-1]
    panel_count = row_count // PANEL
    spread = max(1, row_count // TILE)
    repeat = max(1, TILE // row_count)
    tile_count = lax.axis_size("tile")
    joined = jnp.concatenate([fields[:, 0], fields[:, 1]], axis=-1).astype(jnp.bfloat16)
    panels = inner_factor.reshape(freq_count, panel_count, PANEL, block_count, rank_width)
    products = jnp.einsum(
        "gsbik,gsbq->igskq",
        panels,
        joined.reshape(freq_count, panel_count, PANEL, 2 * focal_count),
        preferred_element_type=jnp.float32,
    )
    rounded = combine(products, signum).astype(jnp.bfloat16)
    per_tile = (
        rounded.astype(jnp.float32)
        .reshape(block_count, freq_count, spread, panel_count // spread, rank_most, 2 * focal_count)
        .sum(axis=3)
    )
    position = lax.axis_index("tile")
    for bit_level in reversed(range(repeat.bit_length() - 1)):
        halfway = per_tile.shape[-1] // 2
        upper_side = position >> bit_level & 1
        lower_part = per_tile[..., :halfway]
        upper_part = per_tile[..., halfway:]
        retained = jnp.where(upper_side == 0, lower_part, upper_part)
        handed = jnp.where(upper_side == 0, upper_part, lower_part)
        per_tile = retained + from_partner(handed.astype(jnp.bfloat16), "tile", bit_level).astype(
            handed.dtype
        )
    first_block = position * row_count // TILE
    ranks_cols = lax.dynamic_slice_in_dim(ranks_oriented, first_block, spread, axis=2)
    within = jnp.arange(rank_most)[:, None] < jnp.transpose(ranks_cols, (1, 0, 2))[..., None, None]
    ready = jnp.where(within, per_tile, 0.0).astype(jnp.bfloat16)
    outgoing = jnp.repeat(ready, repeat, axis=0)
    return outgoing.reshape(tile_count, spread, freq_count, spread, rank_most, ready.shape[-1])


def finish(incoming, outer_factor, signum):
    row_count = outer_factor.shape[1]
    block_count = outer_factor.shape[2]
    repeat = max(1, TILE // row_count)
    tile_count, spread, freq_count, spread_cols, rank_most, group_width = incoming.shape
    regrouped = incoming.reshape(
        tile_count // repeat, repeat, spread, freq_count, spread_cols, rank_most, group_width
    )
    rounded = jnp.transpose(regrouped, (2, 3, 0, 4, 5, 1, 6)).reshape(
        spread, freq_count, block_count, rank_most, repeat * group_width
    )
    twice_focal = repeat * group_width
    half = twice_focal // 2
    second_half = jnp.concatenate(
        [-signum * rounded[..., half:], signum * rounded[..., :half]], axis=-1
    )
    stacked = jnp.concatenate([rounded, second_half], axis=3)
    outer_rows = outer_factor.reshape(
        freq_count, spread, row_count // spread, block_count * 2 * rank_most
    )
    result = jnp.einsum(
        "gsbm,sgmq->gsbq",
        outer_rows,
        stacked.reshape(spread, freq_count, block_count * 2 * rank_most, twice_focal),
        preferred_element_type=jnp.float32,
    )
    result = result.reshape(freq_count, row_count, twice_focal)
    return jnp.stack([result[..., :half], result[..., half:]], axis=1)


def kernel(inner_factor, outer_factor, ranks_oriented, signum, fields):
    incoming = lax.all_to_all(
        prepare(inner_factor, fields, signum, ranks_oriented),
        "tile",
        split_axis=0,
        concat_axis=0,
        tiled=True,
    )
    return finish(incoming, outer_factor, signum)


def mute_pass(spectra, window, inverse, forward):
    gathered = lax.all_to_all(spectra, "freq", split_axis=2, concat_axis=0, tiled=True)
    stacked = gathered.reshape(2 * FREQS, gathered.shape[2] * gathered.shape[3])
    in_time = jnp.dot(inverse, stacked, precision=lax.Precision.HIGHEST)
    kept_mask = jnp.arange(SAMPLES)[:, None] < window.reshape(1, -1)
    muted = jnp.where(kept_mask, in_time, 0.0)
    spectrum = jnp.dot(forward, muted, precision=lax.Precision.HIGHEST).reshape(gathered.shape)
    return lax.all_to_all(spectrum, "freq", split_axis=0, concat_axis=2, tiled=True)


def shards(left_factor, right_factor, tile_ranks, freq_order, mute_window, direct_wave):
    inverse, forward = transform_tables(freq_order)
    swapped = jnp.swapaxes(tile_ranks, 1, 2)
    focus_plus = direct_wave
    focus_minus = mute_pass(
        kernel(right_factor, left_factor, tile_ranks, 1.0, focus_plus),
        mute_window,
        inverse,
        forward,
    )
    focus_plus = direct_wave + mute_pass(
        kernel(left_factor, right_factor, swapped, -1.0, focus_minus), mute_window, inverse, forward
    )
    return (focus_plus, focus_minus)


def solution(mesh):
    return jax.shard_map(
        shards,
        mesh=mesh,
        in_specs=(
            P("freq", "tile", None, None),
            P("freq", "tile", None, None),
            P("freq", None, None),
            P(),
            P(("tile", "freq"), None),
            P("freq", None, "tile", None),
        ),
        out_specs=(P("freq", None, "tile", None), P("freq", None, "tile", None)),
        check_vma=False,
    )
```

profile of v0, /device:TPU:1, one launch (start us, length us, event | category | flops | bytes accessed | tf_op | source)
XLA Modules:
  0.0 193.9 jit_solution(6713182404702762533)
XLA Ops:
  1.7 3.5 %copy.86 = bf16[2,128,32,128]{1,3,2,0:T(8,128)(2,1)S(1)} copy(bf16[2,128,32,128]{3,2,1,0:T(8,128)(2,1)} %param.7) | data formatting | bytes 4194304 | tf_op args[1]
  11.2 8.7 %collective-permute-start = (bf16[32,2,1,64,64]{4,3,0,1,2:T(8,128)(2,1)}, bf16[32,2,1,64,64]{4,3,0,1,2:T(8,128)(2,1)S(1)}, u32[]{:S(2)}, u32[]{:S(2)}) collective-permute-start(bf16[32,2,1,64,64]{4,3,0,1,2:T(8,128)(2,1)} %select_convert_fusion.3), channel_id=1, source_target_pairs={{0,1},{1,0},{2,3},{3,2},{4,5},{5,4},{6,7},{7,6},{8,9},{9,8},{10,11... | collective-permute-start | bytes 1572872 | tf_op jit(solution)/shard_map/ppermute | solution.py:17
  20.2 2.2 %collective-permute-done = bf16[32,2,1,64,64]{4,3,0,1,2:T(8,128)(2,1)S(1)} collective-permute-done((bf16[32,2,1,64,64]{4,3,0,1,2:T(8,128)(2,1)}, bf16[32,2,1,64,64]{4,3,0,1,2:T(8,128)(2,1)S(1)}, u32[]{:S(2)}, u32[]{:S(2)}) %collective-permute-start) | collective-permute-done | bytes 524320 | tf_op jit(solution)/shard_map/ppermute | solution.py:17
  24.3 2.3 %reshape.284 = bf16[64,2,4096]{2,1,0:T(2,128)(2,1)} reshape(bf16[64,1,1,2,64,64]{5,4,3,2,1,0:T(8,128)(2,1)S(1)} %bitcast.122) | data formatting | bytes 2097152
  26.6 5.3 %all-to-all-start = ((bf16[64,2,4096]{2,1,0:T(2,128)(2,1)}), bf16[64,2,4096]{2,1,0:T(2,128)(2,1)S(1)}, u32[]{:S(2)}, u32[]{:S(2)}) async-start(bf16[64,2,4096]{2,1,0:T(2,128)(2,1)} %reshape.284), calls=%async_computation | async-start | bytes 2097152 | tf_op jit(solution)/shard_map/all_to_all | solution.py:112
  31.9 2.3 %reshape.268 = bf16[2,128,4096]{2,1,0:T(8,128)(2,1)} reshape(bf16[2,128,32,128]{3,2,1,0:T(8,128)(2,1)S(1)} %copy-done.1) | data formatting | bytes 4194304 | tf_op jit(solution)/shard_map/reshape.12
  34.2 25.8 %all-to-all-done = bf16[64,2,4096]{2,1,0:T(2,128)(2,1)S(1)} async-done(((bf16[64,2,4096]{2,1,0:T(2,128)(2,1)}), bf16[64,2,4096]{2,1,0:T(2,128)(2,1)S(1)}, u32[]{:S(2)}, u32[]{:S(2)}) %all-to-all-start) | async-done | bytes 1048608 | tf_op jit(solution)/shard_map/all_to_all | solution.py:112
  61.4 3.5 %copy.88 = bf16[1,2,32,1,64,2,64]{6,5,4,2,1,3,0:T(2,128)(2,1)} copy(bf16[1,2,32,1,64,2,64]{6,4,1,5,2,3,0:T(8,128)(2,1)S(1)} %bitcast.126) | data formatting | bytes 2097152 | tf_op jit(solution)/shard_map/transpose | solution.py:89
  64.9 3.9 %reshape.266 = bf16[1,2,32,64,128]{4,3,2,1,0:T(8,128)(2,1)S(1)} reshape(bf16[1,2,32,1,64,2,64]{6,5,4,2,1,3,0:T(2,128)(2,1)} %copy.88) | data formatting | bytes 2097152 | tf_op jit(solution)/shard_map/reshape | solution.py:89
  72.8 10.0 %all-to-all-start.1 = ((f32[8,1,4096]{2,1,0:T(1,128)}), f32[8,1,4096]{2,1,0:T(1,128)S(1)}, u32[]{:S(2)}, u32[]{:S(2)}) async-start(f32[8,1,4096]{2,1,0:T(1,128)} %reshape.286), calls=%async_computation.1 | async-start | bytes 262144 | tf_op jit(solution)/shard_map/all_to_all | solution.py:123
  83.1 7.8 %all-to-all-done.1 = f32[8,1,4096]{2,1,0:T(1,128)S(1)} async-done(((f32[8,1,4096]{2,1,0:T(1,128)}), f32[8,1,4096]{2,1,0:T(1,128)S(1)}, u32[]{:S(2)}, u32[]{:S(2)}) %all-to-all-start.1) | async-done | bytes 131104 | tf_op jit(solution)/shard_map/all_to_all | solution.py:123
  94.4 3.6 %all-to-all-start.2 = ((f32[8,1,4096]{2,1,0:T(1,128)}), f32[8,1,4096]{2,1,0:T(1,128)S(1)}, u32[]{:S(2)}, u32[]{:S(2)}) async-start(f32[8,1,4096]{2,1,0:T(1,128)} %reshape.288), calls=%async_computation.2 | async-start | bytes 262144 | tf_op jit(solution)/shard_map/all_to_all | solution.py:129
  98.0 3.5 %copy.98 = bf16[2,128,32,128]{1,3,2,0:T(8,128)(2,1)S(1)} copy(bf16[2,128,32,128]{3,2,1,0:T(8,128)(2,1)} %param.6) | data formatting | bytes 4194304 | tf_op args[0]
  101.5 4.1 %all-to-all-done.2 = f32[8,1,4096]{2,1,0:T(1,128)S(1)} async-done(((f32[8,1,4096]{2,1,0:T(1,128)}), f32[8,1,4096]{2,1,0:T(1,128)S(1)}, u32[]{:S(2)}, u32[]{:S(2)}) %all-to-all-start.2) | async-done | bytes 131104 | tf_op jit(solution)/shard_map/all_to_all | solution.py:129
  109.6 5.5 %collective-permute-start.1 = (bf16[32,2,1,64,64]{4,3,0,1,2:T(8,128)(2,1)S(1)}, bf16[32,2,1,64,64]{4,3,0,1,2:T(8,128)(2,1)S(1)}, u32[]{:S(2)}, u32[]{:S(2)}) collective-permute-start(bf16[32,2,1,64,64]{4,3,0,1,2:T(8,128)(2,1)S(1)} %select_convert_fusion.1), channel_id=1, source_target_pairs={{0,1},{1,0},{2,3},{3,2},{4,5},{5,4},{6,7},{7,6},{8,9},{9,8},{10,11... | collective-permute-start | bytes 1572872 | tf_op jit(solution)/shard_map/ppermute | solution.py:17
  119.2 2.3 %reshape.290 = bf16[64,2,4096]{2,1,0:T(2,128)(2,1)} reshape(bf16[64,1,1,2,64,64]{5,4,3,2,1,0:T(8,128)(2,1)S(1)} %bitcast.123) | data formatting | bytes 2097152
  121.6 5.6 %all-to-all-start.3 = ((bf16[64,2,4096]{2,1,0:T(2,128)(2,1)}), bf16[64,2,4096]{2,1,0:T(2,128)(2,1)S(1)}, u32[]{:S(2)}, u32[]{:S(2)}) async-start(bf16[64,2,4096]{2,1,0:T(2,128)(2,1)} %reshape.290), calls=%async_computation.3 | async-start | bytes 2097152 | tf_op jit(solution)/shard_map/all_to_all | solution.py:112
  127.2 2.3 %reshape.273 = bf16[2,128,4096]{2,1,0:T(8,128)(2,1)} reshape(bf16[2,128,32,128]{3,2,1,0:T(8,128)(2,1)S(1)} %copy-done.2) | data formatting | bytes 4194304 | tf_op jit(solution)/shard_map/reshape.50
  129.5 25.8 %all-to-all-done.3 = bf16[64,2,4096]{2,1,0:T(2,128)(2,1)S(1)} async-done(((bf16[64,2,4096]{2,1,0:T(2,128)(2,1)}), bf16[64,2,4096]{2,1,0:T(2,128)(2,1)S(1)}, u32[]{:S(2)}, u32[]{:S(2)}) %all-to-all-start.3) | async-done | bytes 1048608 | tf_op jit(solution)/shard_map/all_to_all | solution.py:112
  156.7 3.5 %copy.100 = bf16[1,2,32,1,64,2,64]{6,5,4,2,1,3,0:T(2,128)(2,1)} copy(bf16[1,2,32,1,64,2,64]{6,4,1,5,2,3,0:T(8,128)(2,1)S(1)} %bitcast.127) | data formatting | bytes 2097152 | tf_op jit(solution)/shard_map/transpose | solution.py:89
  160.2 3.9 %reshape.271 = bf16[1,2,32,64,128]{4,3,2,1,0:T(8,128)(2,1)S(1)} reshape(bf16[1,2,32,1,64,2,64]{6,5,4,2,1,3,0:T(2,128)(2,1)} %copy.100) | data formatting | bytes 2097152 | tf_op jit(solution)/shard_map/reshape | solution.py:89
  167.5 10.2 %all_to_all.76 = f32[8,1,4096]{2,1,0:T(1,128)S(1)} all-to-all(f32[8,1,4096]{2,1,0:T(1,128)S(1)} %reshape.292), channel_id=1, replica_groups=mesh['freq'=8,'tile'=64] {'freq'}, dimensions={0} | all-to-all | bytes 262144 | tf_op jit(solution)/shard_map/all_to_all | solution.py:123
  180.7 3.4 %all-to-all-start.5 = ((f32[8,1,4096]{2,1,0:T(1,128)}), f32[8,1,4096]{2,1,0:T(1,128)S(1)}, u32[]{:S(2)}, u32[]{:S(2)}) async-start(f32[8,1,4096]{2,1,0:T(1,128)} %reshape.294), calls=%async_computation.5 | async-start | bytes 262144 | tf_op jit(solution)/shard_map/all_to_all | solution.py:129
  185.0 7.0 %all-to-all-done.5 = f32[8,1,4096]{2,1,0:T(1,128)S(1)} async-done(((f32[8,1,4096]{2,1,0:T(1,128)}), f32[8,1,4096]{2,1,0:T(1,128)S(1)}, u32[]{:S(2)}, u32[]{:S(2)}) %all-to-all-start.5) | async-done | bytes 131104 | tf_op jit(solution)/shard_map/all_to_all | solution.py:129
  (92 shorter events, 36.6 us)
Async XLA Ops:
  0.6 19.3 %copy-start = (s32[2,32,32]{2,1,0:T(8,128)S(1)}, s32[2,32,32]{2,1,0:T(8,128)}, u32[]{:S(2)}) copy-start(s32[2,32,32]{2,1,0:T(8,128)} %param.8) | copy-start | bytes 24580
  11.2 11.2 %collective-permute-start = (bf16[32,2,1,64,64]{4,3,0,1,2:T(8,128)(2,1)}, bf16[32,2,1,64,64]{4,3,0,1,2:T(8,128)(2,1)S(1)}, u32[]{:S(2)}, u32[]{:S(2)}) collective-permute-start(bf16[32,2,1,64,64]{4,3,0,1,2:T(8,128)(2,1)} %select_convert_fusion.3), channel_id=1, source_target_pairs={{0,1},{1,0},{2,3},{3,2},{4,5},{5,4},{6,7},{7,6},{8,9},{9,8},{10,11... | collective-permute-start | bytes 1572872 | tf_op jit(solution)/shard_map/ppermute | solution.py:17
  26.6 5.3 %copy-start.1 = (bf16[2,128,32,128]{3,2,1,0:T(8,128)(2,1)S(1)}, bf16[2,128,32,128]{3,2,1,0:T(8,128)(2,1)}, u32[]{:S(2)}) copy-start(bf16[2,128,32,128]{3,2,1,0:T(8,128)(2,1)} %param.6) | copy-start | bytes 6291460
  26.6 33.5 %all-to-all-start = ((bf16[64,2,4096]{2,1,0:T(2,128)(2,1)}), bf16[64,2,4096]{2,1,0:T(2,128)(2,1)S(1)}, u32[]{:S(2)}, u32[]{:S(2)}) async-start(bf16[64,2,4096]{2,1,0:T(2,128)(2,1)} %reshape.284), calls=%async_computation | async-start | bytes 2097152 | tf_op jit(solution)/shard_map/all_to_all | solution.py:112
  31.9 2.3 %copy-start.7 = (s32[16]{0:T(128)S(1)}, s32[16]{0:T(128)}, u32[]{:S(2)}) copy-start(s32[16]{0:T(128)} %param.9) | copy-start | bytes 196
  69.1 1.6 copy-start.3
  70.7 12.3 %copy-start.6 = (s32[16,64]{1,0:T(8,128)S(1)}, s32[16,64]{1,0:T(8,128)}, u32[]{:S(2)}) copy-start(s32[16,64]{1,0:T(8,128)} %param.10) | copy-start | bytes 12292
  72.8 18.1 %all-to-all-start.1 = ((f32[8,1,4096]{2,1,0:T(1,128)}), f32[8,1,4096]{2,1,0:T(1,128)S(1)}, u32[]{:S(2)}, u32[]{:S(2)}) async-start(f32[8,1,4096]{2,1,0:T(1,128)} %reshape.286), calls=%async_computation.1 | async-start | bytes 262144 | tf_op jit(solution)/shard_map/all_to_all | solution.py:123
  94.4 11.2 %all-to-all-start.2 = ((f32[8,1,4096]{2,1,0:T(1,128)}), f32[8,1,4096]{2,1,0:T(1,128)S(1)}, u32[]{:S(2)}, u32[]{:S(2)}) async-start(f32[8,1,4096]{2,1,0:T(1,128)} %reshape.288), calls=%async_computation.2 | async-start | bytes 262144 | tf_op jit(solution)/shard_map/all_to_all | solution.py:129
  109.6 7.8 %collective-permute-start.1 = (bf16[32,2,1,64,64]{4,3,0,1,2:T(8,128)(2,1)S(1)}, bf16[32,2,1,64,64]{4,3,0,1,2:T(8,128)(2,1)S(1)}, u32[]{:S(2)}, u32[]{:S(2)}) collective-permute-start(bf16[32,2,1,64,64]{4,3,0,1,2:T(8,128)(2,1)S(1)} %select_convert_fusion.1), channel_id=1, source_target_pairs={{0,1},{1,0},{2,3},{3,2},{4,5},{5,4},{6,7},{7,6},{8,9},{9,8},{10,11... | collective-permute-start | bytes 1572872 | tf_op jit(solution)/shard_map/ppermute | solution.py:17
  121.6 5.6 %copy-start.2 = (bf16[2,128,32,128]{3,2,1,0:T(8,128)(2,1)S(1)}, bf16[2,128,32,128]{3,2,1,0:T(8,128)(2,1)}, u32[]{:S(2)}) copy-start(bf16[2,128,32,128]{3,2,1,0:T(8,128)(2,1)} %param.7) | copy-start | bytes 6291460
  121.6 33.8 %all-to-all-start.3 = ((bf16[64,2,4096]{2,1,0:T(2,128)(2,1)}), bf16[64,2,4096]{2,1,0:T(2,128)(2,1)S(1)}, u32[]{:S(2)}, u32[]{:S(2)}) async-start(bf16[64,2,4096]{2,1,0:T(2,128)(2,1)} %reshape.290), calls=%async_computation.3 | async-start | bytes 2097152 | tf_op jit(solution)/shard_map/all_to_all | solution.py:112
  164.5 1.6 copy-start.4
  178.5 5.6 %copy-start.5 = (f32[2,2,128,64]{2,3,1,0:T(8,128)S(1)}, f32[2,2,128,64]{2,3,1,0:T(8,128)}, u32[]{:S(2)}) copy-start(f32[2,2,128,64]{2,3,1,0:T(8,128)} %param.11) | copy-start | bytes 393220
  180.7 11.3 %all-to-all-start.5 = ((f32[8,1,4096]{2,1,0:T(1,128)}), f32[8,1,4096]{2,1,0:T(1,128)S(1)}, u32[]{:S(2)}, u32[]{:S(2)}) async-start(f32[8,1,4096]{2,1,0:T(1,128)} %reshape.294), calls=%async_computation.5 | async-start | bytes 262144 | tf_op jit(solution)/shard_map/all_to_all | solution.py:129
where the time goes:
time: 197 us; the launch traced here: 194 us
  waiting for transfers between devices  74.9 us (38%)
  local copies, waits for them, and re-layouts  44.8 us (23%)
  starting transfers between devices  42.2 us (21%)
  other arithmetic  15.7 us (8%)
  blocking collectives  10.2 us (5%)
  matrix products  4.84 us (2%)
    all_to_all x2, waiting for transfers between devices, kernel(): lax.all_to_all(prepare(inner_factor, fields, signum, ranks_oriented), 'ti...  51.6 us
    unnamed x34, local copies, waits for them, and re-layouts  22.2 us
    ppermute x2, starting transfers between devices, from_partner(): return lax.ppermute(value, axis, pairs)  14.3 us
    all_to_all x2, waiting for transfers between devices, mute_pass(): lax.all_to_all(spectrum, 'freq', split_axis=0, concat_axis=2, tiled=True)  11.1 us
    all_to_all x2, starting transfers between devices, kernel(): lax.all_to_all(prepare(inner_factor, fields, signum, ranks_oriented), 'ti...  10.9 us
    all_to_all x1, blocking collectives, mute_pass(): lax.all_to_all(spectra, 'freq', split_axis=2, concat_axis=0, tiled=True)  10.2 us
    all_to_all x1, starting transfers between devices, mute_pass(): lax.all_to_all(spectra, 'freq', split_axis=2, concat_axis=0, tiled=True)  10 us
    all_to_all x1, waiting for transfers between devices, mute_pass(): lax.all_to_all(spectra, 'freq', split_axis=2, concat_axis=0, tiled=True)  7.78 us
  transfers between devices with their start and end apart: 7, of which 7 were waited for; matrix products, arithmetic and copies ran while one was open for 5% of the time, Pallas kernels for 0%

commit v1 on v0

v1 whole, which is shorter than its diff:
```python
import functools
import math

import jax
import jax.numpy as jnp
from jax import lax
from jax.experimental import pallas as pl
from jax.experimental.pallas import tpu as pltpu
from jax.sharding import PartitionSpec as P

GRID = {64: (8, 4), 8: (2, 2)}
PITCH = 40
ROWS = 128
LANES = 128
HALF = 64
MESH = pl.DeviceIdType.MESH


def roll_half(value):
    return jnp.concatenate([value[:, HALF:], value[:, :HALF]], axis=1)


def kernel(
    dims,
    right_hbm,
    left_hbm,
    ranks_hbm,
    order_hbm,
    window_hbm,
    direct_hbm,
    plus_hbm,
    minus_hbm,
    raw,
    spread,
    right_all,
    left_all,
    right_out,
    left_out,
    direct,
    window,
    ranks,
    order,
    joined,
    joined_out,
    partial,
    sent_a,
    sent_b,
    got_a,
    got_b,
    total,
    image_a,
    image_b,
    gathered_a,
    gathered_b,
    weights,
    samples,
    muted_a,
    muted_b,
    focus,
    swap_out,
    swap_in,
    final,
    minus_stage,
    plus_stage,
    raw_sem,
    in_sem,
    out_sem,
    pair_send,
    pair_recv,
    right_send,
    right_recv,
    left_send,
    left_recv,
    tile_send_a,
    tile_recv_a,
    tile_send_b,
    tile_recv_b,
    freq_send_a,
    freq_recv_a,
    freq_send_b,
    freq_recv_b,
    back_send_a,
    back_recv_a,
    back_send_b,
    back_recv_b,
):
    ny, nx, nz, samples_count = dims
    blocks = ny * nx
    slots = 2 * nz
    rows_each = ROWS // nz
    depth = lax.axis_index("freq")
    tile = lax.axis_index("tile")
    core = lax.rem(tile, 2)
    other = 1 - core
    chip = tile // 2
    chip_y = chip // nx
    chip_x = lax.rem(chip, nx)

    def to_tile(index):
        return {"freq": depth, "tile": index}

    def local(source, target, sem):
        return pltpu.make_async_copy(source, target, sem)

    def remote(source, target, send, recv, device):
        return pltpu.make_async_remote_copy(
            src_ref=source,
            dst_ref=target,
            send_sem=send,
            recv_sem=recv,
            device_id=device,
            device_id_type=MESH,
        )

    partner = {"freq": depth, "tile": tile + other - core}

    small = [
        local(direct_hbm, direct, in_sem.at[0]),
        local(window_hbm, window, in_sem.at[1]),
        local(ranks_hbm, ranks, in_sem.at[2]),
        local(order_hbm, order, in_sem.at[3]),
    ]
    raws = [
        local(right_hbm.at[0], raw.at[0], raw_sem.at[0]),
        local(right_hbm.at[1], raw.at[1], raw_sem.at[1]),
        local(left_hbm.at[0], raw.at[2], raw_sem.at[2]),
        local(left_hbm.at[1], raw.at[3], raw_sem.at[3]),
    ]
    for copy in small[:1] + raws[:2] + small[1:] + raws[2:]:
        copy.start()

    barrier = pltpu.get_barrier_semaphore()

    def greet_tile(index, carry):
        @pl.when(index != chip)
        def _():
            pl.semaphore_signal(
                barrier, inc=1, device_id=to_tile(index * 2 + core), device_id_type=MESH
            )

        return carry

    def greet_freq(index, carry):
        @pl.when(jnp.logical_or(index // 2 != depth, lax.rem(index, 2) != core))
        def _():
            pl.semaphore_signal(
                barrier,
                inc=1,
                device_id={"freq": index // 2, "tile": chip * 2 + lax.rem(index, 2)},
                device_id_type=MESH,
            )

        return carry

    lax.fori_loop(0, blocks, greet_tile, 0)
    lax.fori_loop(0, slots, greet_freq, 0)

    def reorder(slot, target):
        def widen(row, carry):
            for step in range(4):
                spread[pl.ds((row * 4 + step) * PITCH, blocks), :] = raw[
                    slot, row * 4 + step
                ].astype(jnp.float32)
            return carry

        lax.fori_loop(0, ROWS // 4, widen, 0)

        def narrow(index, carry):
            target[index] = spread[pl.ds(index, ROWS, stride=PITCH), :].astype(jnp.bfloat16)
            return carry

        lax.fori_loop(0, blocks, narrow, 0)

    small[0].wait()
    joined_out[...] = jnp.concatenate([direct[other, 0], direct[other, 1]], axis=0).astype(
        jnp.bfloat16
    )
    joined[core] = jnp.concatenate([direct[core, 0], direct[core, 1]], axis=0).astype(jnp.bfloat16)
    raws[0].wait()
    raws[1].wait()
    reorder(other, right_out)
    reorder(core, right_all.at[core])

    lane = lax.broadcasted_iota(jnp.int32, (HALF, LANES), 1)
    low = lane < HALF
    column = lax.rem(lane, HALF)

    def products(fields, factors, side, first, signum):
        wide = jnp.concatenate([factors[side, first + step] for step in range(nx)], axis=1)
        result = jnp.dot(fields, wide, preferred_element_type=jnp.float32)
        pieces = []
        for step in range(nx):
            real = result[:HALF, step * LANES : (step + 1) * LANES]
            turned = roll_half(result[HALF:, step * LANES : (step + 1) * LANES])
            if signum > 0:
                piece = jnp.where(low, real - turned, turned + real)
            else:
                piece = jnp.where(low, real + turned, turned - real)
            pieces.append(piece.astype(jnp.bfloat16))
        return pieces

    def row_of(step, sign):
        reach = ny // 2 - (step + 1) // 2
        offset = jnp.where(lax.rem(step, 2) == 1, reach, ny - reach)
        return lax.rem(chip_y + ny + sign * offset, ny)

    own_fields = joined[core]

    def own_group(step, carry):
        first = step * nx
        pieces = products(own_fields, right_all, core, first, 1.0)
        for index in range(nx):
            partial[first + index] = pieces[index]
        return carry

    lax.fori_loop(0, ny, own_group, 0)

    pl.semaphore_wait(barrier, blocks - 1 + slots - 1)

    pair = remote(joined_out, joined.at[core], pair_send.at[0], pair_recv.at[0], partner)
    pair.start()

    def factor_copy(step, source, target, send, recv):
        first = row_of(step, 1) * nx
        return remote(
            source.at[pl.ds(first, nx)],
            target.at[core, pl.ds(first, nx)],
            send.at[step],
            recv.at[step],
            partner,
        )

    def start_right(step, carry):
        factor_copy(step, right_out, right_all, right_send, right_recv).start()
        return carry

    lax.fori_loop(0, ny, start_right, 0)
    for copy in small[1:]:
        copy.wait()
    pair_in = remote(joined_out, joined.at[other], pair_send.at[0], pair_recv.at[0], partner)
    pair_in.wait_recv()

    def tile_copy(block, source, target, send, recv):
        return remote(
            source.at[block],
            target.at[chip],
            send.at[block],
            recv.at[chip],
            to_tile(block * 2 + core),
        )

    def emit(first, pieces, sent, got, send, recv, rank_of):
        for index in range(nx):
            block = first + index
            kept = jnp.where(column < rank_of(block), pieces[index], 0.0).astype(jnp.bfloat16)
            sent[block] = kept

            @pl.when(block == chip)
            def _():
                got[chip] = kept

        for index in range(nx):
            block = first + index

            @pl.when(block != chip)
            def _():
                tile_copy(block, sent, got, send, recv).start()

    def forward_group(step, carry):
        first = row_of(step, 1) * nx
        remote(
            right_out.at[pl.ds(first, nx)],
            right_all.at[other, pl.ds(first, nx)],
            right_send.at[step],
            right_recv.at[step],
            partner,
        ).wait_recv()
        pieces = products(joined[other], right_all, other, first, 1.0)
        summed = [
            pieces[index].astype(jnp.float32) + partial[first + index].astype(jnp.float32)
            for index in range(nx)
        ]
        emit(
            first,
            summed,
            sent_a,
            got_a,
            tile_send_a,
            tile_recv_a,
            lambda block: ranks[core, block, chip],
        )
        return carry

    lax.fori_loop(0, ny, forward_group, 0)

    raws[2].wait()
    raws[3].wait()
    reorder(2 + other, left_out)

    def start_left(step, carry):
        factor_copy(step, left_out, left_all, left_send, left_recv).start()
        return carry

    lax.fori_loop(0, ny, start_left, 0)
    reorder(2 + core, left_all.at[core])

    turn = 2 * samples_count
    moment = lax.broadcasted_iota(jnp.int32, (samples_count, LANES), 0)
    shift = jnp.where(
        lax.broadcasted_iota(jnp.int32, (samples_count, LANES), 1) < HALF, 0, samples_count // 2
    )

    def weight(slot, carry):
        phase = lax.rem(moment * (2 * order[slot] + 1) + shift, turn)
        weights[slot] = jnp.cos(phase.astype(jnp.float32) * (2.0 * math.pi / turn))
        return carry

    lax.fori_loop(0, slots, weight, 0)

    def wait_left(step, carry):
        first = row_of(step, 1) * nx
        remote(
            left_out.at[pl.ds(first, nx)],
            left_all.at[other, pl.ds(first, nx)],
            left_send.at[step],
            left_recv.at[step],
            partner,
        ).wait_recv()
        return carry

    lax.fori_loop(0, ny, wait_left, 0)

    side_low = lax.broadcasted_iota(jnp.int32, (HALF, LANES), 1) < HALF

    def finish(sent, got, send, recv, factors, signum):
        top_sign = jnp.where(side_low, 1.0, -signum)
        bottom_sign = jnp.where(side_low, 1.0, signum)

        def group(step, carry):
            first = row_of(step, -1) * nx
            for index in range(nx):
                block = first + index

                @pl.when(block != chip)
                def _():
                    remote(
                        sent.at[block],
                        got.at[block],
                        send.at[block],
                        recv.at[block],
                        partner,
                    ).wait_recv()

            columns = []
            for index in range(nx):
                piece = got[first + index].astype(jnp.float32)
                both = jnp.concatenate(
                    [piece * top_sign, roll_half(piece) * bottom_sign], axis=0
                )
                columns.append(both.astype(jnp.bfloat16))
            wide = jnp.concatenate(columns, axis=1)
            for side in range(2):
                rows = jnp.concatenate(
                    [factors[side, first + index] for index in range(nx)], axis=1
                )
                value = lax.dot_general(
                    rows, wide, (((1,), (1,)), ((), ())), preferred_element_type=jnp.float32
                )
                total[side] = total[side] + value
            return carry

        total[...] = jnp.zeros_like(total)
        lax.fori_loop(0, ny, group, 0)

    def to_owner(index, image, gathered, send, recv):
        return remote(
            image.at[index],
            gathered.at[2 * depth + core],
            send.at[index],
            recv.at[2 * depth + core],
            {"freq": lax.rem(index, nz), "tile": chip * 2 + index // nz},
        )

    def spread_image(image, gathered, send, recv):
        image[...] = total[...].reshape(slots, rows_each, LANES).astype(jnp.bfloat16)
        mine = core * nz + depth

        def one(step, carry):
            index = lax.rem(step // nz * nz + lax.rem(step + depth + nz // 2, nz), slots)

            @pl.when(index != mine)
            def _():
                to_owner(index, image, gathered, send, recv).start()

            return carry

        lax.fori_loop(0, slots, one, 0)
        gathered[2 * depth + core] = image[mine]

        def arrive(slot, carry):
            @pl.when(slot != 2 * depth + core)
            def _():
                remote(
                    image.at[0], gathered.at[slot], send.at[0], recv.at[slot], partner
                ).wait_recv()

            return carry

        lax.fori_loop(0, slots, arrive, 0)

    kept = jnp.concatenate([window[...], window[...]], axis=1)

    def mute(gathered, muted):
        values = [gathered[slot].astype(jnp.float32) for slot in range(slots)]

        def invert(step, carry):
            sums = values[0] * weights[0, pl.ds(step, 1), :]
            for slot in range(1, slots):
                sums = sums + values[slot] * weights[slot, pl.ds(step, 1), :]
            sums = (sums + roll_half(sums)) * (2.0 / samples_count)
            samples[step] = jnp.where(step < kept, sums, 0.0)
            return carry

        lax.fori_loop(0, samples_count, invert, 0)

        def forward(slot, carry):
            sums = samples[0] * weights[slot, pl.ds(0, 1), :]
            for step in range(1, samples_count):
                sums = sums + samples[step] * weights[slot, pl.ds(step, 1), :]
            muted[slot // 2, lax.rem(slot, 2)] = sums.astype(jnp.bfloat16)
            return carry

        lax.fori_loop(0, slots, forward, 0)

    finish(sent_a, got_a, tile_send_a, tile_recv_a, left_all, 1.0)
    spread_image(image_a, gathered_a, freq_send_a, freq_recv_a)
    mute(gathered_a, muted_a)

    def to_slot(level, side):
        return remote(
            muted_a.at[level, side],
            focus.at[core * nz + depth],
            back_send_a.at[level * 2 + side],
            back_recv_a.at[core * nz + depth],
            {"freq": level, "tile": chip * 2 + side},
        )

    def send_back(step, carry):
        level = lax.rem(step // 2 + depth + nz // 2, nz)
        side = lax.rem(step, 2)

        @pl.when(jnp.logical_or(level != depth, side != core))
        def _():
            to_slot(level, side).start()

        return carry

    lax.fori_loop(0, slots, send_back, 0)
    focus[core * nz + depth] = muted_a[depth, core]

    def wait_back(index, carry):
        @pl.when(index != core * nz + depth)
        def _():
            remote(
                muted_a.at[0, 0],
                focus.at[index],
                back_send_a.at[0],
                back_recv_a.at[index],
                partner,
            ).wait_recv()

        return carry

    lax.fori_loop(0, slots, wait_back, 0)

    turned = [
        focus[pl.ds(side * nz, nz)].reshape(ROWS, LANES).astype(jnp.float32).T for side in range(2)
    ]
    fields = [value.astype(jnp.bfloat16) for value in turned]

    def backward_group(step, carry):
        first = row_of(step, 1) * nx
        lower = products(fields[0], left_all, 0, first, -1.0)
        upper = products(fields[1], left_all, 1, first, -1.0)
        summed = [
            lower[index].astype(jnp.float32) + upper[index].astype(jnp.float32)
            for index in range(nx)
        ]
        emit(
            first,
            summed,
            sent_b,
            got_b,
            tile_send_b,
            tile_recv_b,
            lambda block: ranks[core, chip, block],
        )
        return carry

    lax.fori_loop(0, ny, backward_group, 0)

    swap_out[0] = fields[0]
    swap_out[1] = fields[1]
    swap = remote(swap_out.at[other], swap_in, pair_send.at[1], pair_recv.at[1], partner)
    swap.start()
    swap.wait_recv()
    own = swap_out[core].astype(jnp.float32)
    minus_stage[core, 0] = own[:HALF]
    minus_stage[core, 1] = own[HALF:]
    theirs = swap_in[...].astype(jnp.float32)
    minus_stage[other, 0] = theirs[:HALF]
    minus_stage[other, 1] = theirs[HALF:]
    minus_copy = local(minus_stage, minus_hbm, out_sem.at[0])
    minus_copy.start()

    finish(sent_b, got_b, tile_send_b, tile_recv_b, right_all, -1.0)
    spread_image(image_b, gathered_b, freq_send_b, freq_recv_b)
    mute(gathered_b, muted_b)

    def to_level(level):
        return remote(
            muted_b.at[level],
            final.at[depth],
            back_send_b.at[level],
            back_recv_b.at[depth],
            {"freq": level, "tile": tile},
        )

    def send_final(step, carry):
        level = lax.rem(step + depth + nz // 2, nz)

        @pl.when(level != depth)
        def _():
            to_level(level).start()

        return carry

    lax.fori_loop(0, nz, send_final, 0)
    final[depth] = muted_b[depth]

    def wait_final(index, carry):
        @pl.when(index != depth)
        def _():
            remote(
                muted_b.at[0],
                final.at[index],
                back_send_b.at[0],
                back_recv_b.at[index],
                partner,
            ).wait_recv()

        return carry

    lax.fori_loop(0, nz, wait_final, 0)
    for slot in range(2):
        value = final[:, slot].reshape(ROWS, LANES).astype(jnp.float32).T
        plus_stage[slot, 0] = direct[slot, 0] + value[:HALF]
        plus_stage[slot, 1] = direct[slot, 1] + value[HALF:]
    plus_copy = local(plus_stage, plus_hbm, out_sem.at[1])
    plus_copy.start()

    pair.wait_send()
    swap.wait_send()

    def drain_factors(step, carry):
        factor_copy(step, right_out, right_all, right_send, right_recv).wait_send()
        factor_copy(step, left_out, left_all, left_send, left_recv).wait_send()
        return carry

    lax.fori_loop(0, ny, drain_factors, 0)

    def drain_tiles(block, carry):
        @pl.when(block != chip)
        def _():
            tile_copy(block, sent_a, got_a, tile_send_a, tile_recv_a).wait_send()
            tile_copy(block, sent_b, got_b, tile_send_b, tile_recv_b).wait_send()

        return carry

    lax.fori_loop(0, blocks, drain_tiles, 0)

    def drain_freq(index, carry):
        @pl.when(index != core * nz + depth)
        def _():
            to_owner(index, image_a, gathered_a, freq_send_a, freq_recv_a).wait_send()
            to_owner(index, image_b, gathered_b, freq_send_b, freq_recv_b).wait_send()

        return carry

    lax.fori_loop(0, slots, drain_freq, 0)

    def drain_back(index, carry):
        level = index // 2
        side = lax.rem(index, 2)

        @pl.when(jnp.logical_or(level != depth, side != core))
        def _():
            to_slot(level, side).wait_send()

        return carry

    lax.fori_loop(0, slots, drain_back, 0)

    def drain_final(level, carry):
        @pl.when(level != depth)
        def _():
            to_level(level).wait_send()

        return carry

    lax.fori_loop(0, nz, drain_final, 0)
    minus_copy.wait()
    plus_copy.wait()


def shards(dims, left_factor, right_factor, tile_ranks, freq_order, mute_window, direct_wave):
    ny, nx, nz, samples_count = dims
    blocks = ny * nx
    slots = 2 * nz
    rows_each = ROWS // nz
    bf16, f32 = jnp.bfloat16, jnp.float32
    dma = pltpu.SemaphoreType.DMA
    turned = jnp.transpose(direct_wave, (0, 1, 3, 2))
    factor = (2, blocks, ROWS, LANES)
    tiles = (blocks, HALF, LANES)
    pieces = (slots, rows_each, LANES)
    stage = (2, 2, HALF, ROWS)
    scratch = [
        pltpu.VMEM((4, ROWS, blocks, LANES), bf16),
        pltpu.VMEM((ROWS * PITCH, LANES), f32),
        pltpu.VMEM(factor, bf16),
        pltpu.VMEM(factor, bf16),
        pltpu.VMEM(factor[1:], bf16),
        pltpu.VMEM(factor[1:], bf16),
        pltpu.VMEM(stage, f32),
        pltpu.VMEM(mute_window.shape, jnp.int32),
        pltpu.SMEM(tile_ranks.shape, jnp.int32),
        pltpu.SMEM(freq_order.shape, jnp.int32),
        pltpu.VMEM((2, LANES, ROWS), bf16),
        pltpu.VMEM((LANES, ROWS), bf16),
        pltpu.VMEM(tiles, bf16),
        pltpu.VMEM(tiles, bf16),
        pltpu.VMEM(tiles, bf16),
        pltpu.VMEM(tiles, bf16),
        pltpu.VMEM(tiles, bf16),
        pltpu.VMEM((2, ROWS, LANES), f32),
        pltpu.VMEM(pieces, bf16),
        pltpu.VMEM(pieces, bf16),
        pltpu.VMEM(pieces, bf16),
        pltpu.VMEM(pieces, bf16),
        pltpu.VMEM((slots, samples_count, LANES), f32),
        pltpu.VMEM((samples_count, rows_each, LANES), f32),
        pltpu.VMEM((nz, 2, rows_each, LANES), bf16),
        pltpu.VMEM((nz, 2, rows_each, LANES), bf16),
        pltpu.VMEM(pieces, bf16),
        pltpu.VMEM((2, LANES, ROWS), bf16),
        pltpu.VMEM((LANES, ROWS), bf16),
        pltpu.VMEM((nz, 2, rows_each, LANES), bf16),
        pltpu.VMEM(stage, f32),
        pltpu.VMEM(stage, f32),
        dma((4,)),
        dma((4,)),
        dma((2,)),
        dma((2,)),
        dma((2,)),
        dma((ny,)),
        dma((ny,)),
        dma((ny,)),
        dma((ny,)),
        dma((blocks,)),
        dma((blocks,)),
        dma((blocks,)),
        dma((blocks,)),
        dma((slots,)),
        dma((slots,)),
        dma((slots,)),
        dma((slots,)),
        dma((slots,)),
        dma((slots,)),
        dma((nz,)),
        dma((nz,)),
    ]
    out = jax.ShapeDtypeStruct(stage, f32)
    plus, minus = pl.pallas_call(
        functools.partial(kernel, dims),
        out_shape=(out, out),
        in_specs=[pl.BlockSpec(memory_space=pl.ANY)] * 6,
        out_specs=(pl.BlockSpec(memory_space=pl.ANY),) * 2,
        scratch_shapes=scratch,
        compiler_params=pltpu.CompilerParams(
            collective_id=0, has_side_effects=True, vmem_limit_bytes=48 * 1024 * 1024
        ),
        name="focusing",
    )(right_factor, left_factor, tile_ranks, freq_order, mute_window, turned)
    return jnp.transpose(plus, (0, 1, 3, 2)), jnp.transpose(minus, (0, 1, 3, 2))


def solution(mesh):
    nz = mesh.shape["freq"]
    ny, nx = GRID[mesh.shape["tile"]]
    dims = (ny, nx, nz, 4 * nz)
    return jax.shard_map(
        functools.partial(shards, dims),
        mesh=mesh,
        in_specs=(
            P("freq", "tile", None, None),
            P("freq", "tile", None, None),
            P("freq", None, None),
            P(),
            P(("tile", "freq"), None),
            P("freq", None, "tile", None),
        ),
        out_specs=(P("freq", None, "tile", None), P("freq", None, "tile", None)),
        check_vma=False,
    )
```

time: 197 us -> 87.2 us (0.44); the launches traced: 194 us -> 86.9 us
  Pallas kernels: 0 us -> 78.8 us
  waiting for transfers between devices: 74.9 us -> 0 us
  starting transfers between devices: 42.2 us -> 0 us
  local copies, waits for them, and re-layouts: 44.8 us -> 7.5 us
  other arithmetic: 15.7 us -> 0 us
  blocking collectives: 10.2 us -> 0 us
  matrix products: 4.84 us -> 0 us
    pallas_call x0 -> x1, Pallas kernels: none -> 78.8 us  [shards(): pl.pallas_call(functools.partial(kernel, dims), out_shape=(out, out), in_...]
    all_to_all x5 -> x0, waiting for transfers between devices: 70.6 us -> none  [the longest x2 51.6 us: kernel(): lax.all_to_all(prepare(inner_factor, fields, signum, ranks_oriented), 'ti...]
    all_to_all x5 -> x0, starting transfers between devices: 27.9 us -> none  [the longest x2 10.9 us: kernel(): lax.all_to_all(prepare(inner_factor, fields, signum, ranks_oriented), 'ti...]
    unnamed x34 -> x14, local copies, waits for them, and re-layouts: 22.2 us -> 7.5 us
    ppermute x2 -> x0, starting transfers between devices: 14.3 us -> none  [from_partner(): return lax.ppermute(value, axis, pairs)]
    all_to_all x1 -> x0, blocking collectives: 10.2 us -> none  [mute_pass(): lax.all_to_all(spectra, 'freq', split_axis=2, concat_axis=0, tiled=True)]
    reshape x4 -> x0, local copies, waits for them, and re-layouts: 8.02 us -> none  [the longest x2 7.77 us: finish(): jnp.transpose(regrouped, (2, 3, 0, 4, 5, 1, 6))]
    transpose x3 -> x0, local copies, waits for them, and re-layouts: 7.13 us -> none  [the longest x2 6.95 us: finish(): jnp.transpose(regrouped, (2, 3, 0, 4, 5, 1, 6))]
  transfers between devices with their start and end apart: 7 -> 0, of which waited for: 7 -> 0; matrix products, arithmetic and copies ran while one was open for 5% -> 0% of each run, Pallas kernels for 0% -> 0%
where the time goes in v1:
time: 87.2 us; the launch traced here: 86.9 us
  Pallas kernels  78.8 us (90%)
  local copies, waits for them, and re-layouts  7.5 us (9%)
    pallas_call x1, Pallas kernels, shards(): pl.pallas_call(functools.partial(kernel, dims), out_shape=(out, out), in_...  78.8 us
    unnamed x14, local copies, waits for them, and re-layouts  7.5 us

profile of v1, /device:TPU:1, one launch (start us, length us, event | category | flops | bytes accessed | tf_op | source)
XLA Modules:
  0.0 86.9 jit_solution(10091614900731988215)
XLA Ops:
  0.6 0.0 copy-start
  0.6 1.6 %copy-done = bf16[2,128,32,128]{3,2,1,0:T(8,128)(2,1)S(1)} copy-done((bf16[2,128,32,128]{3,2,1,0:T(8,128)(2,1)S(1)}, bf16[2,128,32,128]{3,2,1,0:T(8,128)(2,1)}, u32[]{:S(2)}) %copy-start) | copy-done | bytes 2097176
  2.2 0.0 copy-start.1
  2.2 1.6 %copy-done.1 = bf16[2,128,32,128]{3,2,1,0:T(8,128)(2,1)S(1)} copy-done((bf16[2,128,32,128]{3,2,1,0:T(8,128)(2,1)S(1)}, bf16[2,128,32,128]{3,2,1,0:T(8,128)(2,1)}, u32[]{:S(2)}) %copy-start.1) | copy-done | bytes 2097176
  3.8 0.0 copy-start.2
  3.8 0.9 %copy-done.2 = f32[2,2,128,64]{2,3,1,0:T(8,128)S(1)} copy-done((f32[2,2,128,64]{2,3,1,0:T(8,128)S(1)}, f32[2,2,128,64]{2,3,1,0:T(8,128)}, u32[]{:S(2)}) %copy-start.2) | copy-done | bytes 131096
  4.7 0.0 copy-start.3
  4.7 0.8 copy-done.3
  5.5 0.0 copy-start.4
  5.5 0.7 copy-done.4
  6.2 0.0 copy-start.5
  6.2 0.7 copy-done.5
  6.8 78.8 %focusing.1 = (f32[2,2,64,128]{3,2,1,0:T(8,128)S(1)}, f32[2,2,64,128]{3,2,1,0:T(8,128)S(1)}) custom-call(bf16[2,128,32,128]{3,2,1,0:T(8,128)(2,1)S(1)} %copy-done, bf16[2,128,32,128]{3,2,1,0:T(8,128)(2,1)S(1)} %copy-done.1, s32[2,32,32]{2,1,0:T(8,128)S(1)} %copy-done.3, s32[16]{0:T(128)S(1)} %copy-done.5, s32[16,64]{1,0:T(8,128)S(1)} %copy-done.4, ...), custom_call_target="tpu_custom_call" | custom-call | tf_op jit(solution)/shard_map/focusing/pallas_call | solution.py:684
  85.6 0.7 copy.10
  86.3 0.7 copy.11
Async XLA Ops:
  0.6 1.6 %copy-start = (bf16[2,128,32,128]{3,2,1,0:T(8,128)(2,1)S(1)}, bf16[2,128,32,128]{3,2,1,0:T(8,128)(2,1)}, u32[]{:S(2)}) copy-start(bf16[2,128,32,128]{3,2,1,0:T(8,128)(2,1)} %right_hbm.1) | copy-start | bytes 6291460
  2.2 1.6 %copy-start.1 = (bf16[2,128,32,128]{3,2,1,0:T(8,128)(2,1)S(1)}, bf16[2,128,32,128]{3,2,1,0:T(8,128)(2,1)}, u32[]{:S(2)}) copy-start(bf16[2,128,32,128]{3,2,1,0:T(8,128)(2,1)} %left_hbm.1) | copy-start | bytes 6291460
  3.8 0.9 %copy-start.2 = (f32[2,2,128,64]{2,3,1,0:T(8,128)S(1)}, f32[2,2,128,64]{2,3,1,0:T(8,128)}, u32[]{:S(2)}) copy-start(f32[2,2,128,64]{2,3,1,0:T(8,128)} %param.11) | copy-start | bytes 393220
  4.7 0.8 copy-start.3
  5.5 0.7 copy-start.4
  6.2 0.7 copy-start.5

commit v2 on v1

v2 whole, which is shorter than its diff:
```python
import functools
import math

import jax
import jax.numpy as jnp
from jax import lax
from jax.experimental import pallas as pl
from jax.experimental.pallas import tpu as pltpu
from jax.sharding import PartitionSpec as P

GRID = {64: (8, 4), 8: (2, 2)}
PITCH = 40
CHUNKS = 2
FOCAL = 64
PART = FOCAL // CHUNKS
CHUNKS = 2
FOCAL = 64
PART = FOCAL // CHUNKS
CHUNKS = 2
FOCAL = 64
PART = FOCAL // CHUNKS
CHUNKS = 2
FOCAL = 64
PART = FOCAL // CHUNKS
ROWS = 128
LANES = 128
HALF = 64
MESH = pl.DeviceIdType.MESH


def roll_half(value):
    return pltpu.roll(value, HALF, 1)


def kernel(
    dims,
    right_hbm,
    left_hbm,
    ranks_hbm,
    order_hbm,
    window_hbm,
    direct_hbm,
    plus_hbm,
    minus_hbm,
    raw,
    spread,
    right_all,
    left_all,
    right_out,
    left_out,
    direct,
    window,
    limits,
    ranks,
    order,
    joined,
    joined_out,
    partial,
    sent,
    got,
    total,
    image,
    gathered,
    weights,
    samples,
    muted,
    focus,
    swap_out,
    swap_in,
    final,
    minus_stage,
    plus_stage,
    raw_sem,
    in_sem,
    out_sem,
    pair_send,
    pair_recv,
    swap_send,
    swap_recv,
    right_send,
    right_recv,
    left_send,
    left_recv,
    tile_send,
    tile_recv,
    freq_send,
    freq_recv,
    back_send,
    back_recv,
):
    ny, nx, nz, samples_count = dims
    blocks = ny * nx
    slots = 2 * nz
    rows_each = ROWS // nz
    steps = samples_count // CHUNKS
    depth = lax.axis_index("freq")
    tile = lax.axis_index("tile")
    core = lax.rem(tile, 2)
    other = 1 - core
    chip = tile // 2
    chip_y = chip // nx
    chip_x = lax.rem(chip, nx)
    partner = {"freq": depth, "tile": tile + other - core}
    mine = core * nz + depth
    slot_here = 2 * depth + core

    def local(source, target, sem):
        return pltpu.make_async_copy(source, target, sem)

    def remote(source, target, send, recv, device):
        return pltpu.make_async_remote_copy(
            src_ref=source,
            dst_ref=target,
            send_sem=send,
            recv_sem=recv,
            device_id=device,
            device_id_type=MESH,
        )

    small = [
        local(direct_hbm, direct, in_sem.at[0]),
        local(window_hbm, window, in_sem.at[1]),
        local(ranks_hbm, ranks, in_sem.at[2]),
        local(order_hbm, order, in_sem.at[3]),
    ]
    raws = [
        local(right_hbm.at[0], raw.at[0], raw_sem.at[0]),
        local(right_hbm.at[1], raw.at[1], raw_sem.at[1]),
        local(left_hbm.at[0], raw.at[2], raw_sem.at[2]),
        local(left_hbm.at[1], raw.at[3], raw_sem.at[3]),
    ]
    barrier = pltpu.get_barrier_semaphore()

    def greet_tile(index, carry):
        @pl.when(index != chip)
        def _():
            pl.semaphore_signal(
                barrier,
                inc=1,
                device_id={"freq": depth, "tile": index * 2 + core},
                device_id_type=MESH,
            )

        return carry

    def greet_freq(index, carry):
        @pl.when(jnp.logical_or(index // 2 != depth, lax.rem(index, 2) != core))
        def _():
            pl.semaphore_signal(
                barrier,
                inc=1,
                device_id={"freq": index // 2, "tile": chip * 2 + lax.rem(index, 2)},
                device_id_type=MESH,
            )

        return carry

    for copy in raws[:2] + small + raws[2:]:
        copy.start()
    lax.fori_loop(0, blocks, greet_tile, 0)
    lax.fori_loop(0, slots, greet_freq, 0)

    def reorder(slot, target):
        def widen(row, carry):
            for step in range(8):
                spread[pl.ds((row * 8 + step) * PITCH, blocks), :] = raw[
                    slot, row * 8 + step
                ].astype(jnp.float32)
            return carry

        lax.fori_loop(0, ROWS // 8, widen, 0)

        def narrow(index, carry):
            for step in range(2):
                target[index * 2 + step] = spread[
                    pl.ds(index * 2 + step, ROWS, stride=PITCH), :
                ].astype(jnp.bfloat16)
            return carry

        lax.fori_loop(0, blocks // 2, narrow, 0)

    raws[0].wait()
    raws[1].wait()
    reorder(other, right_out)
    reorder(core, right_all.at[core])
    small[0].wait()
    joined_out[...] = jnp.concatenate([direct[other, 0], direct[other, 1]], axis=0).astype(
        jnp.bfloat16
    )
    joined[core] = jnp.concatenate([direct[core, 0], direct[core, 1]], axis=0).astype(jnp.bfloat16)
    pl.semaphore_wait(barrier, blocks - 1 + slots - 1)

    lane = lax.broadcasted_iota(jnp.int32, (HALF, LANES), 1)
    column = lax.rem(lane, HALF)

    def products(fields, factors, side, first, signum):
        count = fields.shape[0] // 2
        low = lax.broadcasted_iota(jnp.int32, (count, LANES), 1) < HALF
        wide = jnp.concatenate([factors[side, first + step] for step in range(nx)], axis=1)
        result = jnp.dot(fields, wide, preferred_element_type=jnp.float32)
        pieces = []
        for step in range(nx):
            real = result[:count, step * LANES : (step + 1) * LANES]
            turned = roll_half(result[count:, step * LANES : (step + 1) * LANES])
            if signum > 0:
                piece = jnp.where(low, real - turned, turned + real)
            else:
                piece = jnp.where(low, real + turned, turned - real)
            pieces.append(piece.astype(jnp.bfloat16))
        return pieces

    def row_of(step, sign):
        reach = ny // 2 - (step + 1) // 2
        offset = jnp.where(lax.rem(step, 2) == 1, reach, ny - reach)
        return lax.rem(chip_y + ny + sign * offset, ny)

    def block_of(first, step):
        offsets = [*range(nx // 2, 0, -1), *range(nx // 2 + 1, nx), 0]
        return first + lax.rem(chip_x + offsets[step], nx)

    pair = remote(joined_out, joined.at[core], pair_send, pair_recv, partner)

    def factor_copy(step, source, target, send, recv):
        first = row_of(step, 1) * nx
        return remote(
            source.at[pl.ds(first, nx)],
            target.at[core, pl.ds(first, nx)],
            send,
            recv.at[step],
            partner,
        )

    def factor_wait(step, source, target, send, recv):
        first = row_of(step, 1) * nx
        remote(
            source.at[pl.ds(first, nx)],
            target.at[other, pl.ds(first, nx)],
            send,
            recv.at[step],
            partner,
        ).wait_recv()

    def start_right(step, carry):
        factor_copy(step, right_out, right_all, right_send, right_recv).start()
        return carry

    pair.start()
    lax.fori_loop(0, ny, start_right, 0)
    own_fields = joined[core]

    def own_group(index, carry):
        for step in range(2):
            first = (index * 2 + step) * nx
            pieces = products(own_fields, right_all, core, first, 1.0)
            for position in range(nx):
                partial[first + position] = pieces[position]
        return carry

    lax.fori_loop(0, ny // 2, own_group, 0)
    for copy in small[1:]:
        copy.wait()
    remote(joined_out, joined.at[other], pair_send, pair_recv, partner).wait_recv()

    def tile_copy(block, phase, part):
        where = pl.ds(part * PART, PART)
        return remote(
            sent.at[phase, block, where],
            got.at[phase, chip, where],
            tile_send.at[phase, part],
            tile_recv.at[phase, part, chip],
            {"freq": depth, "tile": block * 2 + core},
        )

    def send_group(first, phase, part):
        for step in range(nx):
            block = block_of(first, step)

            @pl.when(block != chip)
            def _():
                tile_copy(block, phase, part).start()

    other_fields = joined[other]

    def forward_group(index, carry):
        for inner in range(2):
            factor_wait(index * 2 + inner, right_out, right_all, right_send, right_recv)
        for inner in range(2):
            first = row_of(index * 2 + inner, 1) * nx
            pieces = products(other_fields, right_all, other, first, 1.0)
            for position in range(nx):
                block = first + position
                summed = pieces[position].astype(jnp.float32) + partial[block].astype(jnp.float32)
                value = jnp.where(column < ranks[core, block, chip], summed, 0.0)
                sent[0, block] = value.astype(jnp.bfloat16)
        for inner in range(2):
            send_group(row_of(index * 2 + inner, 1) * nx, 0, 0)
        return carry

    lax.fori_loop(0, ny // 2, forward_group, 0)
    got[0, chip] = sent[0, chip]
    for part in range(1, CHUNKS):

        def forward_rest(step, carry, part=part):
            send_group(row_of(step, 1) * nx, 0, part)
            return carry

        lax.fori_loop(0, ny, forward_rest, 0)
    raws[2].wait()
    raws[3].wait()
    reorder(2 + other, left_out)

    def start_left(step, carry):
        factor_copy(step, left_out, left_all, left_send, left_recv).start()
        return carry

    lax.fori_loop(0, ny, start_left, 0)
    reorder(2 + core, left_all.at[core])
    turn = 2 * samples_count
    place = lax.broadcasted_iota(jnp.int32, (steps, LANES), 1)
    moment = lax.broadcasted_iota(jnp.int32, (steps, LANES), 0) * CHUNKS + lax.rem(
        place // PART, CHUNKS
    )
    shift = jnp.where(place < HALF, 0, samples_count // 2)

    def weight(slot, carry):
        phase = lax.rem(moment * (2 * order[slot] + 1) + shift, turn)
        weights[slot] = jnp.cos(phase.astype(jnp.float32) * (2.0 * math.pi / turn))
        return carry

    lax.fori_loop(0, slots, weight, 0)
    late = lax.rem(lax.broadcasted_iota(jnp.int32, (rows_each, LANES), 1) // PART, CHUNKS)
    for part in range(CHUNKS):
        lane_window = window[:, part * PART : (part + 1) * PART]
        limits[part] = jnp.concatenate([lane_window] * (LANES // PART), axis=1) - late

    def wait_left(step, carry):
        factor_wait(step, left_out, left_all, left_send, left_recv)
        return carry

    lax.fori_loop(0, ny, wait_left, 0)

    def finish(phase, part, factors, signum):
        where = slice(part * PART, (part + 1) * PART)
        side_low = lax.broadcasted_iota(jnp.int32, (PART, LANES), 1) < HALF
        top_sign = jnp.where(side_low, 1.0, -signum)
        bottom_sign = jnp.where(side_low, 1.0, signum)

        def group(index, carry):
            members = []
            for inner in range(span):
                first = row_of(index * span + inner, -1) * nx
                members += [first + position for position in range(nx)]
            for block in members:

                @pl.when(block != chip)
                def _(block=block):
                    remote(
                        sent.at[phase, block, where],
                        got.at[phase, block, where],
                        tile_send.at[phase, part],
                        tile_recv.at[phase, part, block],
                        partner,
                    ).wait_recv()

            columns = []
            for block in members:
                piece = got[phase, block, where].astype(jnp.float32)
                top = (piece * top_sign).astype(jnp.bfloat16)
                bottom = (roll_half(piece) * bottom_sign).astype(jnp.bfloat16)
                columns.append(jnp.concatenate([top] * CHUNKS + [bottom] * CHUNKS, axis=0))
            wide = jnp.concatenate(columns, axis=1)
            for side in range(2):
                rows = jnp.concatenate([factors[side, block] for block in members], axis=1)
                value = lax.dot_general(
                    rows, wide, (((1,), (1,)), ((), ())), preferred_element_type=jnp.float32
                )
                total[side] = total[side] + value
            return carry

        span = max(1, ny // 2)
        total[...] = jnp.zeros_like(total)
        lax.fori_loop(0, ny // span, group, 0)

    def to_owner(index, phase, part):
        return remote(
            image.at[phase, part, index],
            gathered.at[phase, part, slot_here],
            freq_send.at[phase, part],
            freq_recv.at[phase, part],
            {"freq": lax.rem(index, nz), "tile": chip * 2 + index // nz},
        )

    def spread_image(phase, part):
        image[phase, part] = total[...].reshape(slots, rows_each, LANES).astype(jnp.bfloat16)

        def one(step, carry):
            level = lax.rem(step + depth + nz // 2, nz)
            for side in range(2):

                @pl.when(jnp.logical_or(level != depth, side != core))
                def _():
                    to_owner(side * nz + level, phase, part).start()

            return carry

        lax.fori_loop(0, nz, one, 0)
        gathered[phase, part, slot_here] = image[phase, part, mine]

    def many(source, target, send, recv, count):
        return remote(source.at[pl.ds(0, count)], target.at[pl.ds(0, count)], send, recv, partner)

    def freq_many(phase, part):
        return many(
            image.at[phase, part],
            gathered.at[phase, part],
            freq_send.at[phase, part],
            freq_recv.at[phase, part],
            slots - 1,
        )

    def mute(phase, part):
        limit = limits[part]
        values = [gathered[phase, part, slot].astype(jnp.float32) for slot in range(slots)]

        many_steps = min(8, steps)

        def invert(index, carry):
            for inner in range(many_steps):
                step = index * many_steps + inner
                sums = values[0] * weights[0, pl.ds(step, 1), :]
                for slot in range(1, slots):
                    sums = sums + values[slot] * weights[slot, pl.ds(step, 1), :]
                sums = (sums + roll_half(sums)) * (2.0 / samples_count)
                samples[step] = jnp.where(step * CHUNKS < limit, sums, 0.0)
            return carry

        lax.fori_loop(0, steps // many_steps, invert, 0)

        many_slots = min(8, slots)

        def forward(index, carry):
            for inner in range(many_slots):
                slot = index * many_slots + inner
                sums = samples[0] * weights[slot, pl.ds(0, 1), :]
                for step in range(1, steps):
                    sums = sums + samples[step] * weights[slot, pl.ds(step, 1), :]
                for group in range(1, CHUNKS):
                    sums = sums + pltpu.roll(sums, LANES - group * PART, 1)
                muted[phase, part, slot] = sums.astype(jnp.bfloat16)
            return carry

        lax.fori_loop(0, slots // many_slots, forward, 0)

    def to_slot(level, side, part):
        return remote(
            muted.at[0, part, level * 2 + side],
            focus.at[part, mine],
            back_send.at[0, part],
            back_recv.at[0, part],
            {"freq": level, "tile": chip * 2 + side},
        )

    def send_back(part):
        def one(step, carry):
            level = lax.rem(step + depth + nz // 2, nz)
            for side in range(2):

                @pl.when(jnp.logical_or(level != depth, side != core))
                def _():
                    to_slot(level, side, part).start()

            return carry

        lax.fori_loop(0, nz, one, 0)
        focus[part, mine] = muted[0, part, slot_here]

    def back_many(part):
        return many(
            muted.at[0, part],
            focus.at[part],
            back_send.at[0, part],
            back_recv.at[0, part],
            slots - 1,
        )

    def valid_rows(value):
        return jnp.concatenate([value[:PART], value[HALF : HALF + PART]], axis=0)

    def backward(part):
        fields = []
        for side in range(2):
            value = focus[part, side * nz : (side + 1) * nz].reshape(ROWS, LANES)
            fields.append(valid_rows(value.astype(jnp.float32).T).astype(jnp.bfloat16))
            swap_out[part, side] = fields[side]

        def one(index, carry):
            for inner in range(2):
                first = row_of(index * 2 + inner, 1) * nx
                lower = products(fields[0], left_all, 0, first, -1.0)
                upper = products(fields[1], left_all, 1, first, -1.0)
                for position in range(nx):
                    block = first + position
                    summed = lower[position].astype(jnp.float32)
                    summed = summed + upper[position].astype(jnp.float32)
                    kept = column[:PART] < ranks[core, chip, block]
                    value = jnp.where(kept, summed, 0.0).astype(jnp.bfloat16)
                    sent[1, block, slice(part * PART, (part + 1) * PART)] = value
            for inner in range(2):
                send_group(row_of(index * 2 + inner, 1) * nx, 1, part)
            return carry

        lax.fori_loop(0, ny // 2, one, 0)
        where = slice(part * PART, (part + 1) * PART)
        got[1, chip, where] = sent[1, chip, where]

    def swap(part):
        return remote(
            swap_out.at[part, other],
            swap_in.at[part],
            swap_send.at[part],
            swap_recv.at[part],
            partner,
        )

    def to_level(level, part):
        return remote(
            muted.at[1, part, pl.ds(level * 2, 2)],
            final.at[part, pl.ds(depth * 2, 2)],
            back_send.at[1, part],
            back_recv.at[1, part],
            {"freq": level, "tile": tile},
        )

    def send_final(part):
        def one(step, carry):
            level = lax.rem(step + depth + nz // 2, nz)

            @pl.when(level != depth)
            def _():
                to_level(level, part).start()

            return carry

        lax.fori_loop(0, nz, one, 0)
        final[part, pl.ds(depth * 2, 2)] = muted[1, part, pl.ds(depth * 2, 2)]

    def final_many(part):
        return many(
            muted.at[1, part],
            final.at[part],
            back_send.at[1, part],
            back_recv.at[1, part],
            slots - 2,
        )

    def tile_many(phase, part):
        where = pl.ds(part * PART, PART)
        return remote(
            sent.at[phase, pl.ds(0, blocks - 1), where],
            got.at[phase, pl.ds(0, blocks - 1), where],
            tile_send.at[phase, part],
            tile_recv.at[phase, part, 0],
            partner,
        )

    def store_plus(part):
        where = slice(part * PART, (part + 1) * PART)
        for slot in range(2):
            value = jnp.concatenate([final[part, 2 * level + slot] for level in range(nz)], axis=0)
            value = valid_rows(value.astype(jnp.float32).T).astype(plus_stage.dtype)
            plus_stage[slot, 0, where] = value[:PART]
            plus_stage[slot, 1, where] = value[PART:]

    for part in range(CHUNKS):
        finish(0, part, left_all, 1.0)
        spread_image(0, part)
        if part > 0:
            back_many(part - 1).wait_recv()
            backward(part - 1)
        freq_many(0, part).wait_recv()
        mute(0, part)
        send_back(part)
    back_many(CHUNKS - 1).wait_recv()
    backward(CHUNKS - 1)
    for part in range(CHUNKS):
        finish(1, part, right_all, -1.0)
        spread_image(1, part)
        if part > 0:
            final_many(part - 1).wait_recv()
            store_plus(part - 1)
            tile_many(1, part - 1).wait_send()
        if part == 0:
            for piece in range(CHUNKS):
                swap(piece).start()
            for piece in range(CHUNKS):
                rows = slice(piece * PART, (piece + 1) * PART)
                own = swap_out[piece, core]
                minus_stage[core, 0, rows] = own[:PART]
                minus_stage[core, 1, rows] = own[PART:]
                swap(piece).wait_recv()
                theirs = swap_in[piece]
                minus_stage[other, 0, rows] = theirs[:PART]
                minus_stage[other, 1, rows] = theirs[PART:]
            minus_copy = local(minus_stage, minus_hbm, out_sem.at[0])
            minus_copy.start()
            for piece in range(CHUNKS):
                tile_many(0, piece).wait_send()
                freq_many(0, piece).wait_send()
                back_many(piece).wait_send()
                swap(piece).wait_send()
            pair.wait_send()
            remote(right_out, right_all.at[core], right_send, right_recv.at[0], partner).wait_send()
            remote(left_out, left_all.at[core], left_send, left_recv.at[0], partner).wait_send()
        freq_many(1, part).wait_recv()
        mute(1, part)
        send_final(part)
    tile_many(1, CHUNKS - 1).wait_send()
    for part in range(CHUNKS):
        freq_many(1, part).wait_send()
    minus_copy.wait()
    final_many(CHUNKS - 1).wait_recv()
    store_plus(CHUNKS - 1)
    plus_copy = local(plus_stage, plus_hbm, out_sem.at[1])
    plus_copy.start()
    for part in range(CHUNKS):
        final_many(part).wait_send()
    plus_copy.wait()


def shards(dims, left_factor, right_factor, tile_ranks, freq_order, mute_window, direct_wave):
    ny, nx, nz, samples_count = dims
    blocks = ny * nx
    slots = 2 * nz
    rows_each = ROWS // nz
    bf16, f32 = jnp.bfloat16, jnp.float32
    dma = pltpu.SemaphoreType.DMA
    turned = jnp.transpose(direct_wave, (0, 1, 3, 2))
    factor = (2, blocks, ROWS, LANES)
    tiles = (blocks, FOCAL, LANES)
    pieces = (2, CHUNKS, slots, rows_each, LANES)
    stage = (2, 2, FOCAL, ROWS)
    each = (2, CHUNKS)
    scratch = [
        pltpu.VMEM((4, ROWS, blocks, LANES), bf16),
        pltpu.VMEM((ROWS * PITCH, LANES), f32),
        pltpu.VMEM(factor, bf16),
        pltpu.VMEM(factor, bf16),
        pltpu.VMEM(factor[1:], bf16),
        pltpu.VMEM(factor[1:], bf16),
        pltpu.VMEM(stage, f32),
        pltpu.VMEM(mute_window.shape, jnp.int32),
        pltpu.VMEM((CHUNKS, rows_each, LANES), jnp.int32),
        pltpu.SMEM(tile_ranks.shape, jnp.int32),
        pltpu.SMEM(freq_order.shape, jnp.int32),
        pltpu.VMEM((2, LANES, ROWS), bf16),
        pltpu.VMEM((LANES, ROWS), bf16),
        pltpu.VMEM(tiles, bf16),
        pltpu.VMEM((2,) + tiles, bf16),
        pltpu.VMEM((2,) + tiles, bf16),
        pltpu.VMEM((2, ROWS, LANES), f32),
        pltpu.VMEM(pieces, bf16),
        pltpu.VMEM(pieces, bf16),
        pltpu.VMEM((slots, samples_count // CHUNKS, LANES), f32),
        pltpu.VMEM((samples_count // CHUNKS, rows_each, LANES), f32),
        pltpu.VMEM(pieces, bf16),
        pltpu.VMEM(pieces[1:], bf16),
        pltpu.VMEM((CHUNKS, 2, 2 * PART, ROWS), bf16),
        pltpu.VMEM((CHUNKS, 2 * PART, ROWS), bf16),
        pltpu.VMEM(pieces[1:], bf16),
        pltpu.VMEM(stage, bf16),
        pltpu.VMEM(stage, bf16),
        dma((4,)),
        dma((4,)),
        dma((2,)),
        dma,
        dma,
        dma((CHUNKS,)),
        dma((CHUNKS,)),
        dma,
        dma((ny,)),
        dma,
        dma((ny,)),
        dma(each),
        dma(each + (blocks,)),
        dma(each),
        dma(each),
        dma(each),
        dma(each),
    ]
    out = jax.ShapeDtypeStruct(stage, bf16)
    plus, minus = pl.pallas_call(
        functools.partial(kernel, dims),
        out_shape=(out, out),
        in_specs=[pl.BlockSpec(memory_space=pltpu.HBM)] * 6,
        out_specs=(pl.BlockSpec(memory_space=pl.ANY),) * 2,
        scratch_shapes=scratch,
        compiler_params=pltpu.CompilerParams(
            collective_id=0, has_side_effects=True, vmem_limit_bytes=66000000
        ),
        name="focusing",
    )(right_factor, left_factor, tile_ranks, freq_order, mute_window, turned)
    plus = jnp.transpose(turned + plus.astype(f32), (0, 1, 3, 2))
    return plus, jnp.transpose(minus.astype(f32), (0, 1, 3, 2))


def solution(mesh):
    nz = mesh.shape["freq"]
    ny, nx = GRID[mesh.shape["tile"]]
    dims = (ny, nx, nz, 4 * nz)
    return jax.shard_map(
        functools.partial(shards, dims),
        mesh=mesh,
        in_specs=(
            P("freq", "tile", None, None),
            P("freq", "tile", None, None),
            P("freq", None, None),
            P(),
            P(("tile", "freq"), None),
            P("freq", None, "tile", None),
        ),
        out_specs=(P("freq", None, "tile", None), P("freq", None, "tile", None)),
        check_vma=False,
    )
```

time: 87.2 us -> 71.6 us (0.82)
  Pallas kernels: 78.8 us -> 67.8 us
  local copies, waits for them, and re-layouts: 7.5 us -> 0.01 us
  other arithmetic: 0 us -> 3.02 us
    pallas_call x1, Pallas kernels: 78.8 us -> 67.8 us  [shards(): pl.pallas_call(functools.partial(kernel, dims), out_shape=(out, out), in_...]
    unnamed x14 -> x2, local copies, waits for them, and re-layouts: 7.5 us -> 0.01 us
    transpose x0 -> x2, other arithmetic: none -> 3.02 us  [the longest x1 1.51 us: shards(): plus = jnp.transpose(turned + plus.astype(f32), (0, 1, 3, 2))]
where the time goes in v2:
time: 71.6 us; the launch traced here: 71.4 us
  Pallas kernels  67.8 us (95%)
  other arithmetic  3.02 us (4%)
    pallas_call x1, Pallas kernels, shards(): pl.pallas_call(functools.partial(kernel, dims), out_shape=(out, out), in_...  67.8 us
    transpose x1, other arithmetic, shards(): plus = jnp.transpose(turned + plus.astype(f32), (0, 1, 3, 2))  1.51 us
    transpose x1, other arithmetic, shards(): return (plus, jnp.transpose(minus.astype(f32), (0, 1, 3, 2)))  1.5 us

profile of v2, /device:TPU:1, one launch (start us, length us, event | category | flops | bytes accessed | tf_op | source)
XLA Modules:
  0.0 71.4 jit_solution(6116006319752068303)
XLA Ops:
  0.6 0.0 copy-start
  0.6 67.8 %focusing.1 = (bf16[2,2,64,128]{3,2,1,0:T(8,128)(2,1)}, bf16[2,2,64,128]{3,2,1,0:T(8,128)(2,1)}) custom-call(bf16[2,128,32,128]{3,2,1,0:T(8,128)(2,1)} %right_hbm.1, bf16[2,128,32,128]{3,2,1,0:T(8,128)(2,1)} %left_hbm.1, s32[2,32,32]{2,1,0:T(8,128)} %ranks_hbm.1, s32[16]{0:T(128)} %order_hbm.1, s32[16,64]{1,0:T(8,128)} %window_hbm.1, f32[2,2,64,128]{3,2,1,0:T(8,128)} %bitcast.6), custom_call_target="tpu_custom_call" | custom-call | tf_op jit(solution)/shard_map/focusing/pallas_call | solution.py:691
  68.4 0.0 copy-done
  68.4 1.5 %add_bitcast_fusion = f32[2,2,128,64]{2,3,1,0:T(8,128)} fusion(bf16[2,2,64,128]{3,2,1,0:T(8,128)(2,1)} %get-tuple-element.4, f32[2,2,128,64]{2,3,1,0:T(8,128)S(1)} %copy-done), kind=kLoop, calls=%fused_computation.1 | loop fusion | flops 65536 | bytes 327680 | tf_op jit(solution)/shard_map/transpose | solution.py:702
  69.9 1.5 %convert_bitcast_fusion = f32[2,2,128,64]{2,3,1,0:T(8,128)} fusion(bf16[2,2,64,128]{3,2,1,0:T(8,128)(2,1)} %get-tuple-element.5), kind=kLoop, calls=%fused_computation | loop fusion | flops 32768 | bytes 196608 | tf_op jit(solution)/shard_map/transpose | solution.py:703
Async XLA Ops:
  0.6 67.8 %copy-start = (f32[2,2,128,64]{2,3,1,0:T(8,128)S(1)}, f32[2,2,128,64]{2,3,1,0:T(8,128)}, u32[]{:S(2)}) copy-start(f32[2,2,128,64]{2,3,1,0:T(8,128)} %param.11) | copy-start | bytes 393220

commit v3 on v2

--- a/solution.py
+++ b/solution.py
@@ -40,8 +40,7 @@
     order_hbm,
     window_hbm,
     direct_hbm,
-    plus_hbm,
-    minus_hbm,
+    both_hbm,
     raw,
     spread,
     right_all,
@@ -214,6 +213,10 @@
         offset = jnp.where(lax.rem(step, 2) == 1, reach, ny - reach)
         return lax.rem(chip_y + ny + sign * offset, ny)
 
+    def level_of(step):
+        reach = nz // 2 - (step + 1) // 2
+        return lax.rem(depth + jnp.where(lax.rem(step, 2) == 1, reach, nz - reach), nz)
+
     def block_of(first, step):
         offsets = [*range(nx // 2, 0, -1), *range(nx // 2 + 1, nx), 0]
         return first + lax.rem(chip_x + offsets[step], nx)
@@ -394,7 +397,7 @@
         image[phase, part] = total[...].reshape(slots, rows_each, LANES).astype(jnp.bfloat16)
 
         def one(step, carry):
-            level = lax.rem(step + depth + nz // 2, nz)
+            level = level_of(step)
             for side in range(2):
 
                 @pl.when(jnp.logical_or(level != depth, side != core))
@@ -462,7 +465,7 @@
 
     def send_back(part):
         def one(step, carry):
-            level = lax.rem(step + depth + nz // 2, nz)
+            level = level_of(step)
             for side in range(2):
 
                 @pl.when(jnp.logical_or(level != depth, side != core))
@@ -533,7 +536,7 @@
 
     def send_final(part):
         def one(step, carry):
-            level = lax.rem(step + depth + nz // 2, nz)
+            level = level_of(step)
 
             @pl.when(level != depth)
             def _():
@@ -601,7 +604,7 @@
                 theirs = swap_in[piece]
                 minus_stage[other, 0, rows] = theirs[:PART]
                 minus_stage[other, 1, rows] = theirs[PART:]
-            minus_copy = local(minus_stage, minus_hbm, out_sem.at[0])
+            minus_copy = local(minus_stage, both_hbm.at[1], out_sem.at[0])
             minus_copy.start()
             for piece in range(CHUNKS):
                 tile_many(0, piece).wait_send()
@@ -620,11 +623,34 @@
     minus_copy.wait()
     final_many(CHUNKS - 1).wait_recv()
     store_plus(CHUNKS - 1)
-    plus_copy = local(plus_stage, plus_hbm, out_sem.at[1])
+    plus_copy = local(plus_stage, both_hbm.at[0], out_sem.at[1])
     plus_copy.start()
     for part in range(CHUNKS):
         final_many(part).wait_send()
     plus_copy.wait()
+
+
+def widen_results(both_hbm, direct_hbm, plus_hbm, minus_hbm, both, direct, wide, in_sem, out_sem):
+    ins = [
+        pltpu.make_async_copy(both_hbm.at[1], both.at[1], in_sem.at[0]),
+        pltpu.make_async_copy(both_hbm.at[0], both.at[0], in_sem.at[1]),
+        pltpu.make_async_copy(direct_hbm, direct, in_sem.at[2]),
+    ]
+    outs = [
+        pltpu.make_async_copy(wide.at[1], minus_hbm, out_sem.at[0]),
+        pltpu.make_async_copy(wide.at[0], plus_hbm, out_sem.at[1]),
+    ]
+    for copy in ins:
+        copy.start()
+    ins[0].wait()
+    wide[1] = both[1].astype(jnp.float32)
+    outs[0].start()
+    ins[1].wait()
+    ins[2].wait()
+    wide[0] = direct[...] + both[0].astype(jnp.float32)
+    outs[1].start()
+    for copy in outs:
+        copy.wait()
 
 
 def shards(dims, left_factor, right_factor, tile_ranks, freq_order, mute_window, direct_wave):
@@ -687,20 +713,35 @@
         dma(each),
         dma(each),
     ]
-    out = jax.ShapeDtypeStruct(stage, bf16)
-    plus, minus = pl.pallas_call(
+    out = jax.ShapeDtypeStruct((2,) + stage, bf16)
+    both = pl.pallas_call(
         functools.partial(kernel, dims),
-        out_shape=(out, out),
+        out_shape=out,
         in_specs=[pl.BlockSpec(memory_space=pltpu.HBM)] * 6,
-        out_specs=(pl.BlockSpec(memory_space=pl.ANY),) * 2,
+        out_specs=pl.BlockSpec(memory_space=pl.ANY),
         scratch_shapes=scratch,
         compiler_params=pltpu.CompilerParams(
             collective_id=0, has_side_effects=True, vmem_limit_bytes=66000000
         ),
         name="focusing",
     )(right_factor, left_factor, tile_ranks, freq_order, mute_window, turned)
-    plus = jnp.transpose(turned + plus.astype(f32), (0, 1, 3, 2))
-    return plus, jnp.transpose(minus.astype(f32), (0, 1, 3, 2))
+    wide = jax.ShapeDtypeStruct(stage, f32)
+    plus, minus = pl.pallas_call(
+        widen_results,
+        out_shape=(wide, wide),
+        in_specs=[pl.BlockSpec(memory_space=pl.ANY)] * 2,
+        out_specs=(pl.BlockSpec(memory_space=pl.ANY),) * 2,
+        scratch_shapes=[
+            pltpu.VMEM((2,) + stage, bf16),
+            pltpu.VMEM(stage, f32),
+            pltpu.VMEM((2,) + stage, f32),
+            dma((3,)),
+            dma((2,)),
+        ],
+        compiler_params=pltpu.CompilerParams(vmem_limit_bytes=66000000),
+        name="widen",
+    )(both, turned)
+    return jnp.transpose(plus, (0, 1, 3, 2)), jnp.transpose(minus, (0, 1, 3, 2))
 
 
 def solution(mesh):

time: 71.6 us -> 69 us (0.964)
  other arithmetic: 3.02 us -> 0 us
    transpose x2 -> x0, other arithmetic: 3.02 us -> none  [the longest x1 1.51 us: shards(): plus = jnp.transpose(turned + plus.astype(f32), (0, 1, 3, 2))]
    pallas_call x1 -> x2, Pallas kernels: 67.8 us -> 68.2 us  [the longest x1 66.5 us: shards(): pl.pallas_call(functools.partial(kernel, dims), out_shape=out, in_specs=[...]
where the time goes in v3:
time: 69 us; the launch traced here: 68.8 us
  Pallas kernels  68.2 us (99%)
    pallas_call x1, Pallas kernels, shards(): pl.pallas_call(functools.partial(kernel, dims), out_shape=out, in_specs=[...  66.5 us
    pallas_call x1, Pallas kernels, shards(): pl.pallas_call(widen_results, out_shape=(wide, wide), in_specs=[pl.BlockS...  1.69 us

profile of v3, /device:TPU:1, one launch (start us, length us, event | category | flops | bytes accessed | tf_op | source)
XLA Modules:
  0.0 68.8 jit_solution(12052399510735165634)
XLA Ops:
  0.6 66.5 %focusing.1.both_hbm = bf16[2,2,2,64,128]{4,3,2,1,0:T(8,128)(2,1)} custom-call(bf16[2,128,32,128]{3,2,1,0:T(8,128)(2,1)} %right_hbm.1, bf16[2,128,32,128]{3,2,1,0:T(8,128)(2,1)} %left_hbm.1, s32[2,32,32]{2,1,0:T(8,128)} %ranks_hbm.1, s32[16]{0:T(128)} %order_hbm.1, s32[16,64]{1,0:T(8,128)} %window_hbm.1, f32[2,2,64,128]{3,2,1,0:T(8,128)} %bitcast.3), custom_call_target="tpu_custom_call" | custom-call | tf_op jit(solution)/shard_map/focusing/pallas_call | solution.py:717
  67.1 1.7 %widen.1 = (f32[2,2,64,128]{3,2,1,0:T(8,128)}, f32[2,2,64,128]{3,2,1,0:T(8,128)}) custom-call(bf16[2,2,2,64,128]{4,3,2,1,0:T(8,128)(2,1)} %focusing.1.both_hbm, f32[2,2,64,128]{3,2,1,0:T(8,128)} %bitcast.4), custom_call_target="tpu_custom_call" | custom-call | tf_op jit(solution)/shard_map/widen/pallas_call | solution.py:729

commit v4 on v3

--- a/solution.py
+++ b/solution.py
@@ -130,34 +130,53 @@
     ]
     barrier = pltpu.get_barrier_semaphore()
 
-    def greet_tile(index, carry):
-        @pl.when(index != chip)
-        def _():
-            pl.semaphore_signal(
-                barrier,
-                inc=1,
-                device_id={"freq": depth, "tile": index * 2 + core},
-                device_id_type=MESH,
-            )
+    def row_of(step, sign):
+        reach = ny // 2 - (step + 1) // 2
+        offset = jnp.where(lax.rem(step, 2) == 1, reach, ny - reach)
+        return lax.rem(chip_y + ny + sign * offset, ny)
+
+    def level_of(step):
+        reach = nz // 2 - (step + 1) // 2
+        return lax.rem(depth + jnp.where(lax.rem(step, 2) == 1, reach, nz - reach), nz)
+
+    def block_of(first, step):
+        offsets = [*range(nx // 2, 0, -1), *range(nx // 2 + 1, nx), 0]
+        return first + lax.rem(chip_x + offsets[step], nx)
+
+    def greet_tile(step, carry):
+        for inner in range(nx):
+            block = block_of(row_of(step, 1) * nx, inner)
+
+            @pl.when(block != chip)
+            def _(block=block):
+                pl.semaphore_signal(
+                    barrier,
+                    inc=1,
+                    device_id={"freq": depth, "tile": block * 2 + core},
+                    device_id_type=MESH,
+                )
 
         return carry
 
-    def greet_freq(index, carry):
-        @pl.when(jnp.logical_or(index // 2 != depth, lax.rem(index, 2) != core))
-        def _():
-            pl.semaphore_signal(
-                barrier,
-                inc=1,
-                device_id={"freq": index // 2, "tile": chip * 2 + lax.rem(index, 2)},
-                device_id_type=MESH,
-            )
+    def greet_freq(step, carry):
+        level = level_of(step)
+        for side in range(2):
+
+            @pl.when(jnp.logical_or(level != depth, side != core))
+            def _(side=side):
+                pl.semaphore_signal(
+                    barrier,
+                    inc=1,
+                    device_id={"freq": level, "tile": chip * 2 + side},
+                    device_id_type=MESH,
+                )
 
         return carry
 
     for copy in raws[:2] + small + raws[2:]:
         copy.start()
-    lax.fori_loop(0, blocks, greet_tile, 0)
-    lax.fori_loop(0, slots, greet_freq, 0)
+    lax.fori_loop(0, ny, greet_tile, 0)
+    lax.fori_loop(0, nz, greet_freq, 0)
 
     def reorder(slot, target):
         def widen(row, carry):
@@ -208,19 +227,6 @@
             pieces.append(piece.astype(jnp.bfloat16))
         return pieces
 
-    def row_of(step, sign):
-        reach = ny // 2 - (step + 1) // 2
-        offset = jnp.where(lax.rem(step, 2) == 1, reach, ny - reach)
-        return lax.rem(chip_y + ny + sign * offset, ny)
-
-    def level_of(step):
-        reach = nz // 2 - (step + 1) // 2
-        return lax.rem(depth + jnp.where(lax.rem(step, 2) == 1, reach, nz - reach), nz)
-
-    def block_of(first, step):
-        offsets = [*range(nx // 2, 0, -1), *range(nx // 2 + 1, nx), 0]
-        return first + lax.rem(chip_x + offsets[step], nx)
-
     pair = remote(joined_out, joined.at[core], pair_send, pair_recv, partner)
 
     def factor_copy(step, source, target, send, recv):
@@ -380,7 +386,7 @@
                 total[side] = total[side] + value
             return carry
 
-        span = max(1, ny // 2)
+        span = ny if part == CHUNKS - 1 else max(1, ny // 2)
         total[...] = jnp.zeros_like(total)
         lax.fori_loop(0, ny // span, group, 0)
 
@@ -425,7 +431,7 @@
         limit = limits[part]
         values = [gathered[phase, part, slot].astype(jnp.float32) for slot in range(slots)]
 
-        many_steps = min(8, steps)
+        many_steps = min(16, steps)
 
         def invert(index, carry):
             for inner in range(many_steps):

time: 69 us -> 68.9 us (level)
  no operation moved by 1% of the time
where the time goes in v4:
time: 68.9 us; the launch traced here: 68.8 us
  Pallas kernels  68.1 us (99%)
    pallas_call x1, Pallas kernels, shards(): pl.pallas_call(functools.partial(kernel, dims), out_shape=out, in_specs=[...  66.5 us
    pallas_call x1, Pallas kernels, shards(): pl.pallas_call(widen_results, out_shape=(wide, wide), in_specs=[pl.BlockS...  1.69 us

profile of v4, /device:TPU:1, one launch (start us, length us, event | category | flops | bytes accessed | tf_op | source)
XLA Modules:
  0.0 68.8 jit_solution(17132230600622919175)
XLA Ops:
  0.6 66.5 %focusing.1.both_hbm = bf16[2,2,2,64,128]{4,3,2,1,0:T(8,128)(2,1)} custom-call(bf16[2,128,32,128]{3,2,1,0:T(8,128)(2,1)} %right_hbm.1, bf16[2,128,32,128]{3,2,1,0:T(8,128)(2,1)} %left_hbm.1, s32[2,32,32]{2,1,0:T(8,128)} %ranks_hbm.1, s32[16]{0:T(128)} %order_hbm.1, s32[16,64]{1,0:T(8,128)} %window_hbm.1, f32[2,2,64,128]{3,2,1,0:T(8,128)} %bitcast.3), custom_call_target="tpu_custom_call" | custom-call | tf_op jit(solution)/shard_map/focusing/pallas_call | solution.py:723
  67.1 1.7 %widen.1 = (f32[2,2,64,128]{3,2,1,0:T(8,128)}, f32[2,2,64,128]{3,2,1,0:T(8,128)}) custom-call(bf16[2,2,2,64,128]{4,3,2,1,0:T(8,128)(2,1)} %focusing.1.both_hbm, f32[2,2,64,128]{3,2,1,0:T(8,128)} %bitcast.4), custom_call_target="tpu_custom_call" | custom-call | tf_op jit(solution)/shard_map/widen/pallas_call | solution.py:735
